TPU v7x, 32 devices: a whole 2x2x4 slice. The times are simulated.
32 devices in a mesh: tm: 16 (over z, x, core), mom: 2 (over y).
Axes of the slice: x: 2, y: 2, z: 4, core: 2. Of those that a mesh axis runs over, the one named last changes fastest.
Arguments:
- fields: bfloat16 [16, 4, 2, 512, 512], P('tm', 'mom'), may hold values from -1 to 1
- mom_pairs: int32 [6, 2], P('mom'), may hold values from 0 to 3, as said below
- deltas: int32 [4], replicated, may hold values from 0 to 3, each once
Outputs:
- time_traces: float32 [16, 2, 4, 6], P('tm', None, None, 'mom')
- summed_traces: float32 [2, 4, 6], P(None, None, 'mom')
Inputs may be any that keep to these rules, and one draw needn't show every extreme that they name: `mom_pairs`: column 0 may be any momentum; in row r, column 1 lies in momentum group r // 3, that is from (r // 3) * 2 to (r // 3) * 2 + 1.
All inputs are finite; a program needn't handle non-finite values.
Results may differ from a plain program's by a relative error of at most 0.0003.
Values may be sent and summed in bfloat16 or wider, within the bound.
A program may use at most 128 MiB of HBM per device.

v0:
```python
import jax
import jax.numpy as jnp
from jax import lax
from jax.sharding import PartitionSpec as P


def from_behind(block, axis, distance):
    devices = range(lax.axis_size(axis))
    route = [((i - distance) % len(devices), i) for i in devices]
    return lax.ppermute(block, axis, route)


def products(source, target):
    product_full = jnp.einsum("xij,yjk->xyik", source, target, preferred_element_type=jnp.float32)
    real_part = product_full[0, 0] - product_full[1, 1]
    imag_part = product_full[0, 1] + product_full[1, 0]
    direct = jnp.trace(real_part)
    box_value = jnp.sum(real_part * real_part.T) - jnp.sum(imag_part * imag_part.T)
    return (direct, box_value)


def pair_terms(source_stack, target_stack, target_index):
    directs = []
    boxes = []
    for which in range(source_stack.shape[0]):
        target = lax.dynamic_index_in_dim(target_stack, target_index[which], 0, keepdims=False)
        direct, box_value = products(source_stack[which], target)
        directs.append(direct)
        boxes.append(box_value)
    return jnp.stack([jnp.stack(directs), jnp.stack(boxes)])


def reorder(stacked, deltas):
    picker = (deltas[:, None] == jnp.arange(deltas.shape[0], dtype=jnp.int32)[None, :]).astype(
        jnp.float32
    )
    return jnp.sum(picker[:, :, None] * stacked[..., None, :, :], axis=-2)


def per_device(fields, mom_pairs, deltas):
    group_index = lax.axis_index("mom")
    per_group = fields.shape[1]
    sep_count = deltas.shape[0]
    own_fields = fields[0]
    all_momenta = lax.all_gather(own_fields, "mom", axis=0, tiled=True)
    pair_count = mom_pairs.shape[0]
    sources = jnp.stack(
        [
            lax.dynamic_index_in_dim(all_momenta, mom_pairs[which, 0], 0, keepdims=False)
            for which in range(pair_count)
        ]
    )
    target_index = mom_pairs[:, 1] - group_index * per_group
    raw_terms = []
    local_terms = []
    totals = []

    def record(result):
        totals.append(lax.psum(result, "tm"))
        raw_terms.append(result)

    moving = own_fields
    for separation in range(1, sep_count + 1):
        moving = from_behind(moving, "tm", -1)
        result = pair_terms(sources, moving, target_index)
        record(result)
        local_terms.append(result)
    time_traces = reorder(jnp.stack(local_terms, axis=1), deltas)[None]
    summed = jnp.stack(totals, axis=1)
    summed_traces = reorder(summed, deltas)
    return (time_traces, summed_traces)


def solution(mesh):
    return jax.shard_map(
        per_device,
        mesh=mesh,
        in_specs=(P("tm", "mom", None, None, None), P("mom", None), P()),
        out_specs=(P("tm", None, None, "mom"), P(None, None, "mom")),
        check_vma=False,
    )
```

profile of v0, /device:TPU:0, one launch (start us, length us, event | category | flops | bytes accessed | tf_op | source)
XLA Modules:
  0.0 261.6 jit_solution(1147506468308186212)
XLA Ops:
  7.9 5.5 %collective-permute-start = (bf16[2,2,512,512]{3,2,1,0:T(8,128)(2,1)}, bf16[2,2,512,512]{3,2,1,0:T(8,128)(2,1)}, u32[]{:S(2)}, u32[]{:S(2)}) collective-permute-start(bf16[2,2,512,512]{3,2,1,0:T(8,128)(2,1)} %bitcast.329), channel_id=1, source_target_pairs={{2,0},{4,2},{6,4},{8,6},{10,8},{12,10},{14,12},{16,14},{18,16},{20... | collective-permute-start | bytes 6291464 | tf_op jit(solution)/shard_map/ppermute | solution.py:10
  13.4 23.9 %collective-permute-done = bf16[2,2,512,512]{3,2,1,0:T(8,128)(2,1)} collective-permute-done((bf16[2,2,512,512]{3,2,1,0:T(8,128)(2,1)}, bf16[2,2,512,512]{3,2,1,0:T(8,128)(2,1)}, u32[]{:S(2)}, u32[]{:S(2)}) %collective-permute-start) | collective-permute-done | bytes 2097184 | tf_op jit(solution)/shard_map/ppermute | solution.py:10
  37.3 4.6 %collective-permute-start.1 = (bf16[2,2,512,512]{3,2,1,0:T(8,128)(2,1)}, bf16[2,2,512,512]{3,2,1,0:T(8,128)(2,1)}, u32[]{:S(2)}, u32[]{:S(2)}) collective-permute-start(bf16[2,2,512,512]{3,2,1,0:T(8,128)(2,1)} %collective-permute-done), channel_id=1, source_target_pairs={{2,0},{4,2},{6,4},{8,6},{10,8},{12,10},{14,12},{16,14},{18,16},{20... | collective-permute-start | bytes 6291464 | tf_op jit(solution)/shard_map/ppermute | solution.py:10
  45.6 1.4 fusion.109
  56.3 12.7 %all-gather.3.cloned.1.call-done = bf16[1,4,2,512,512]{4,3,2,0,1:T(8,128)(2,1)} async-done(((bf16[1,2,2,512,512]{4,3,2,0,1:T(8,128)(2,1)}), bf16[1,4,2,512,512]{4,3,2,0,1:T(8,128)(2,1)}) %all-gather.3.cloned.1.call-update) | async-done | bytes 4194320 | tf_op jit(solution)/shard_map/all_gather | solution.py:45
  69.0 2.8 %convolution_bitcast_fusion.11 = f32[2,2,512,512]{2,3,0,1:T(8,128)S(1)} fusion(bf16[2,2,512,512]{3,2,1,0:T(8,128)(2,1)} %collective-permute-done, s32[]{:T(128)S(6)} %select_n.67, bf16[1,4,2,512,512]{4,3,2,0,1:T(8,128)(2,1)} %all-gather.3.cloned.1.call-done, s32[]{:T(128)S(6)} %select_n.68), kind=kOutput, calls=%fused_computation.11 | convolution fusion | flops 1073741824 | bytes 6291464 | tf_op jit(solution)/shard_map/xij,yjk->xyik/dot_general | solution.py:14
  72.3 1.6 copy.110
  73.9 1.3 copy.111
  75.3 3.0 %convolution_bitcast_fusion.10 = f32[2,2,512,512]{2,3,1,0:T(8,128)S(1)} fusion(bf16[2,2,512,512]{3,2,1,0:T(8,128)(2,1)} %collective-permute-done, s32[]{:T(128)S(6)} %select_n.70, bf16[1,4,2,512,512]{4,3,2,0,1:T(8,128)(2,1)} %all-gather.3.cloned.1.call-done, s32[]{:T(128)S(6)} %select_n.71), kind=kOutput, calls=%fused_computation.10 | convolution fusion | flops 1073741824 | bytes 6291464 | tf_op jit(solution)/shard_map/xij,yjk->xyik/dot_general | solution.py:14
  78.3 2.5 convolution_bitcast_fusion.9
  80.8 1.8 fusion.19
  82.6 1.9 fusion.18
  84.5 2.5 convolution_bitcast_fusion.8
  87.0 1.8 fusion.14
  88.8 2.5 convolution_bitcast_fusion.7
  91.4 1.5 fusion.13
  92.9 2.5 convolution_bitcast_fusion.6
  96.0 3.7 %collective-permute-start.2 = (bf16[2,2,512,512]{3,2,1,0:T(8,128)(2,1)}, bf16[2,2,512,512]{3,2,1,0:T(8,128)(2,1)}, u32[]{:S(2)}, u32[]{:S(2)}) collective-permute-start(bf16[2,2,512,512]{3,2,1,0:T(8,128)(2,1)} %collective-permute-done.1), channel_id=1, source_target_pairs={{2,0},{4,2},{6,4},{8,6},{10,8},{12,10},{14,12},{16,14},{18,16},{20... | collective-permute-start | bytes 6291464 | tf_op jit(solution)/shard_map/ppermute | solution.py:10
  100.9 2.5 copy.112
  103.5 2.6 %copy.113 = f32[512,512]{1,0:T(8,128)} copy(f32[512,512]{0,1:T(8,128)} %get-tuple-element.36) | data formatting | bytes 2097152 | tf_op jit(solution)/shard_map/add | solution.py:16
  106.1 2.6 copy.114
  108.7 2.6 copy.115
  111.2 2.5 copy.122
  113.8 2.5 copy.123
  116.3 2.6 copy.124
  118.9 1.3 copy.125
  120.2 1.3 copy.126
  121.5 1.3 copy.127
  124.1 3.3 %select_reduce_fusion.10 = (f32[]{:T(128)}, f32[]{:T(128)}, f32[]{:T(128)}) fusion(f32[512,512]{0,1:T(8,128)} %get-tuple-element.37, f32[512,512]{1,0:T(8,128)} %copy.112, f32[512,512]{0,1:T(8,128)} %get-tuple-element.36, f32[512,512]{1,0:T(8,128)} %copy.113), kind=kLoop, calls=%fused_computation.152 | loop fusion | flops 1835005 | bytes 4194316 | tf_op jit(solution)/shard_map/jit(trace)/reduce_sum | solution.py:17
  128.8 3.3 %select_reduce_fusion.9 = (f32[]{:T(128)}, f32[]{:T(128)}, f32[]{:T(128)}) fusion(f32[512,512]{0,1:T(8,128)} %get-tuple-element.39, f32[512,512]{1,0:T(8,128)} %copy.114, f32[512,512]{0,1:T(8,128)} %get-tuple-element.38, f32[512,512]{1,0:T(8,128)} %copy.115), kind=kLoop, calls=%fused_computation.150 | loop fusion | flops 1835005 | bytes 4194316 | tf_op jit(solution)/shard_map/jit(trace)/reduce_sum | solution.py:17
  133.3 3.3 %select_reduce_fusion.8 = (f32[]{:T(128)}, f32[]{:T(128)}, f32[]{:T(128)}) fusion(f32[512,512]{0,1:T(8,128)} %get-tuple-element.41, f32[512,512]{1,0:T(8,128)} %copy.122, f32[512,512]{0,1:T(8,128)} %get-tuple-element.40, f32[512,512]{1,0:T(8,128)} %copy.123), kind=kLoop, calls=%fused_computation.148 | loop fusion | flops 1835005 | bytes 4194316 | tf_op jit(solution)/shard_map/jit(trace)/reduce_sum | solution.py:17
  137.9 2.9 %select_reduce_fusion.7 = (f32[]{:T(128)}, f32[]{:T(128)}, f32[]{:T(128)}) fusion(f32[512,512]{0,1:T(8,128)} %get-tuple-element.43, f32[512,512]{1,0:T(8,128)} %copy.124, f32[512,512]{0,1:T(8,128)S(1)} %get-tuple-element.42, f32[512,512]{1,0:T(8,128)} %copy.125), kind=kLoop, calls=%fused_computation.146 | loop fusion | flops 1835005 | bytes 4194316 | tf_op jit(solution)/shard_map/jit(trace)/reduce_sum | solution.py:17
  142.1 2.4 select_reduce_fusion.6
  145.9 2.0 maximum_bitcast_fusion.4
  147.9 1.9 maximum_bitcast_fusion.6
  150.0 2.8 %convolution_bitcast_fusion.5 = f32[2,2,512,512]{2,3,1,0:T(8,128)S(1)} fusion(bf16[2,2,512,512]{3,2,1,0:T(8,128)(2,1)} %collective-permute-done.2, s32[]{:T(128)S(6)} %select_n.67, bf16[1,4,2,512,512]{4,3,2,0,1:T(8,128)(2,1)} %all-gather.3.cloned.1.call-done, s32[]{:T(128)S(6)} %select_n.68), kind=kOutput, calls=%fused_computation.5 | convolution fusion | flops 1073741824 | bytes 6291464 | tf_op jit(solution)/shard_map/xij,yjk->xyik/dot_general | solution.py:14
  153.3 1.3 copy.134
  154.7 1.3 copy.135
  156.0 1.4 collective-permute-start.3
  157.4 2.8 %convolution_bitcast_fusion.4 = f32[2,2,512,512]{2,3,1,0:T(8,128)S(1)} fusion(bf16[2,2,512,512]{3,2,1,0:T(8,128)(2,1)} %collective-permute-done.2, s32[]{:T(128)S(6)} %select_n.70, bf16[1,4,2,512,512]{4,3,2,0,1:T(8,128)(2,1)} %all-gather.3.cloned.1.call-done, s32[]{:T(128)S(6)} %select_n.71), kind=kOutput, calls=%fused_computation.4 | convolution fusion | flops 1073741824 | bytes 6291464 | tf_op jit(solution)/shard_map/xij,yjk->xyik/dot_general | solution.py:14
  160.3 1.5 fusion.7
  161.7 2.9 %copy.136 = f32[512,512]{1,0:T(8,128)} copy(f32[512,512]{0,1:T(8,128)} %get-tuple-element.49) | data formatting | bytes 2097152 | tf_op jit(solution)/shard_map/sub | solution.py:15
  165.9 2.8 %convolution_bitcast_fusion.3 = f32[2,2,512,512]{2,3,1,0:T(8,128)S(1)} fusion(bf16[2,2,512,512]{3,2,1,0:T(8,128)(2,1)} %collective-permute-done.2, s32[]{:T(128)S(6)} %select_n.73, bf16[1,4,2,512,512]{4,3,2,0,1:T(8,128)(2,1)} %all-gather.3.cloned.1.call-done, s32[]{:T(128)S(6)} %select_n.74), kind=kOutput, calls=%fused_computation.3 | convolution fusion | flops 1073741824 | bytes 6291464 | tf_op jit(solution)/shard_map/xij,yjk->xyik/dot_general | solution.py:14
  169.3 1.3 copy.138
  170.6 1.4 copy.139
  172.0 2.8 %select_reduce_fusion.5 = (f32[]{:T(128)}, f32[]{:T(128)}, f32[]{:T(128)}) fusion(f32[512,512]{0,1:T(8,128)} %copy-done.5, f32[512,512]{1,0:T(8,128)} %copy.134, f32[512,512]{0,1:T(8,128)S(1)} %get-tuple-element.46, f32[512,512]{1,0:T(8,128)} %copy.135), kind=kLoop, calls=%fused_computation.142 | loop fusion | flops 1835005 | bytes 4194316 | tf_op jit(solution)/shard_map/jit(trace)/reduce_sum | solution.py:17
  176.2 3.4 %select_reduce_fusion.4 = (f32[]{:T(128)}, f32[]{:T(128)}, f32[]{:T(128)}) fusion(f32[512,512]{0,1:T(8,128)} %get-tuple-element.49, f32[512,512]{1,0:T(8,128)} %copy.136, f32[512,512]{0,1:T(8,128)} %copy-done.7, f32[512,512]{1,0:T(8,128)} %copy.137), kind=kLoop, calls=%fused_computation.140 | loop fusion | flops 1835005 | bytes 4194316 | tf_op jit(solution)/shard_map/jit(trace)/reduce_sum | solution.py:17
  180.9 2.3 select_reduce_fusion.3
  184.5 2.0 maximum_bitcast_fusion.8
  186.6 2.9 %convolution_bitcast_fusion.2 = f32[2,2,512,512]{2,3,1,0:T(8,128)S(1)} fusion(bf16[2,2,512,512]{3,2,1,0:T(8,128)(2,1)} %collective-permute-done.3, s32[]{:T(128)S(6)} %select_n.67, bf16[1,4,2,512,512]{4,3,2,0,1:T(8,128)(2,1)} %all-gather.3.cloned.1.call-done, s32[]{:T(128)S(6)} %select_n.68), kind=kOutput, calls=%fused_computation.2 | convolution fusion | flops 1073741824 | bytes 6291464 | tf_op jit(solution)/shard_map/xij,yjk->xyik/dot_general | solution.py:14
  189.9 1.3 copy.146
  191.2 1.3 copy.147
  192.5 2.8 %convolution_bitcast_fusion.1 = f32[2,2,512,512]{2,3,1,0:T(8,128)S(1)} fusion(bf16[2,2,512,512]{3,2,1,0:T(8,128)(2,1)} %collective-permute-done.3, s32[]{:T(128)S(6)} %select_n.70, bf16[1,4,2,512,512]{4,3,2,0,1:T(8,128)(2,1)} %all-gather.3.cloned.1.call-done, s32[]{:T(128)S(6)} %select_n.71), kind=kOutput, calls=%fused_computation.1 | convolution fusion | flops 1073741824 | bytes 6291464 | tf_op jit(solution)/shard_map/xij,yjk->xyik/dot_general | solution.py:14
  195.4 1.5 fusion.1
  196.9 2.6 %copy.148 = f32[512,512]{1,0:T(8,128)} copy(f32[512,512]{0,1:T(8,128)} %get-tuple-element.55) | data formatting | bytes 2097152 | tf_op jit(solution)/shard_map/sub | solution.py:15
  199.5 1.3 copy.149
  200.8 2.8 %convolution_bitcast_fusion = f32[2,2,512,512]{2,3,1,0:T(8,128)S(1)} fusion(bf16[2,2,512,512]{3,2,1,0:T(8,128)(2,1)} %collective-permute-done.3, s32[]{:T(128)S(6)} %select_n.73, bf16[1,4,2,512,512]{4,3,2,0,1:T(8,128)(2,1)} %all-gather.3.cloned.1.call-done, s32[]{:T(128)S(6)} %select_n.74), kind=kOutput, calls=%fused_computation | convolution fusion | flops 1073741824 | bytes 6291464 | tf_op jit(solution)/shard_map/xij,yjk->xyik/dot_general | solution.py:14
  203.7 2.1 fusion
  205.7 2.5 copy.150
  208.3 2.5 copy.151
  210.9 2.7 %select_reduce_fusion.2 = (f32[]{:T(128)}, f32[]{:T(128)}, f32[]{:T(128)}) fusion(f32[512,512]{0,1:T(8,128)S(1)} %get-tuple-element.53, f32[512,512]{1,0:T(8,128)} %copy.146, f32[512,512]{0,1:T(8,128)S(1)} %get-tuple-element.52, f32[512,512]{1,0:T(8,128)} %copy.147), kind=kLoop, calls=%fused_computation.136 | loop fusion | flops 1835005 | bytes 4194316 | tf_op jit(solution)/shard_map/jit(trace)/reduce_sum | solution.py:17
  213.5 2.3 select_reduce_fusion.1
  220.9 1.9 maximum_bitcast_fusion.10
  223.0 30.3 %all-reduce = (f32[2,1,3]{2,0,1:T(2,128)S(1)}, f32[2,1,3]{2,0,1:T(2,128)S(1)}, f32[2,1,3]{2,0,1:T(2,128)S(1)}, f32[2,1,3]{2,0,1:T(2,128)S(1)}) all-reduce(f32[2,1,3]{2,0,1:T(2,128)S(1)} %maximum_bitcast_fusion.3, f32[2,1,3]{2,0,1:T(2,128)S(1)} %maximum_bitcast_fusion.2, ...), channel_id=1, replica_groups=mesh['tm'=16,'mom'=2] {'tm'}, use_global_device_ids=true, to_apply=%region_40.41 | all-reduce | flops 24 | bytes 192 | tf_op jit(solution)/shard_map/psum | solution.py:59
  (63 shorter events, 10.7 us)
Async XLA Ops:
  7.2 61.8 %all-gather.3.cloned.1.call-start = ((), (), s32[]{:S(2)}) async-start(), calls=%async_computation | async-start | bytes 6291456 | tf_op jit(solution)/shard_map/all_gather | solution.py:45
  7.9 29.4 %collective-permute-start = (bf16[2,2,512,512]{3,2,1,0:T(8,128)(2,1)}, bf16[2,2,512,512]{3,2,1,0:T(8,128)(2,1)}, u32[]{:S(2)}, u32[]{:S(2)}) collective-permute-start(bf16[2,2,512,512]{3,2,1,0:T(8,128)(2,1)} %bitcast.329), channel_id=1, source_target_pairs={{2,0},{4,2},{6,4},{8,6},{10,8},{12,10},{14,12},{16,14},{18,16},{20... | collective-permute-start | bytes 6291464 | tf_op jit(solution)/shard_map/ppermute | solution.py:10
  37.3 47.2 %collective-permute-start.1 = (bf16[2,2,512,512]{3,2,1,0:T(8,128)(2,1)}, bf16[2,2,512,512]{3,2,1,0:T(8,128)(2,1)}, u32[]{:S(2)}, u32[]{:S(2)}) collective-permute-start(bf16[2,2,512,512]{3,2,1,0:T(8,128)(2,1)} %collective-permute-done), channel_id=1, source_target_pairs={{2,0},{4,2},{6,4},{8,6},{10,8},{12,10},{14,12},{16,14},{18,16},{20... | collective-permute-start | bytes 6291464 | tf_op jit(solution)/shard_map/ppermute | solution.py:10
  72.3 5.9 %copy-start.1 = (f32[512,512]{0,1:T(8,128)}, f32[512,512]{0,1:T(8,128)S(1)}, u32[]{:S(2)}) copy-start(f32[512,512]{0,1:T(8,128)S(1)} %get-tuple-element.34) | copy-start | bytes 3145732
  72.3 5.9 %copy-start.3 = (f32[512,512]{0,1:T(8,128)}, f32[512,512]{0,1:T(8,128)S(1)}, u32[]{:S(2)}) copy-start(f32[512,512]{0,1:T(8,128)S(1)} %get-tuple-element.35) | copy-start | bytes 3145732
  75.3 3.0 %copy-start = (bf16[1,4,2,512,512]{4,3,2,0,1:T(8,128)(2,1)S(1)}, bf16[1,4,2,512,512]{4,3,2,0,1:T(8,128)(2,1)}, u32[]{:S(2)}) copy-start(bf16[1,4,2,512,512]{4,3,2,0,1:T(8,128)(2,1)} %all-gather.3.cloned.1.call-done) | copy-start | bytes 12582916
  95.4 4.3 %copy-start.2 = (f32[512,512]{0,1:T(8,128)S(1)}, f32[512,512]{0,1:T(8,128)}, u32[]{:S(2)}) copy-start(f32[512,512]{0,1:T(8,128)} %copy-done.1) | copy-start | bytes 3145732
  95.5 4.3 %copy-start.4 = (f32[512,512]{0,1:T(8,128)S(1)}, f32[512,512]{0,1:T(8,128)}, u32[]{:S(2)}) copy-start(f32[512,512]{0,1:T(8,128)} %copy-done.3) | copy-start | bytes 3145732
  95.5 4.3 %copy-start.10 = (f32[512,512]{1,0:T(8,128)S(1)}, f32[512,512]{1,0:T(8,128)}, u32[]{:S(2)}) copy-start(f32[512,512]{1,0:T(8,128)} %copy.110) | copy-start | bytes 3145732
  95.5 4.3 %copy-start.11 = (f32[512,512]{1,0:T(8,128)S(1)}, f32[512,512]{1,0:T(8,128)}, u32[]{:S(2)}) copy-start(f32[512,512]{1,0:T(8,128)} %copy.111) | copy-start | bytes 3145732
  96.0 54.0 %collective-permute-start.2 = (bf16[2,2,512,512]{3,2,1,0:T(8,128)(2,1)}, bf16[2,2,512,512]{3,2,1,0:T(8,128)(2,1)}, u32[]{:S(2)}, u32[]{:S(2)}) collective-permute-start(bf16[2,2,512,512]{3,2,1,0:T(8,128)(2,1)} %collective-permute-done.1), channel_id=1, source_target_pairs={{2,0},{4,2},{6,4},{8,6},{10,8},{12,10},{14,12},{16,14},{18,16},{20... | collective-permute-start | bytes 6291464 | tf_op jit(solution)/shard_map/ppermute | solution.py:10
  153.3 6.9 %copy-start.5 = (f32[512,512]{0,1:T(8,128)}, f32[512,512]{0,1:T(8,128)S(1)}, u32[]{:S(2)}) copy-start(f32[512,512]{0,1:T(8,128)S(1)} %get-tuple-element.47) | copy-start | bytes 3145732
  156.0 30.6 %collective-permute-start.3 = (bf16[2,2,512,512]{3,2,1,0:T(8,128)(2,1)}, bf16[2,2,512,512]{3,2,1,0:T(8,128)(2,1)}, u32[]{:S(2)}, u32[]{:S(2)}) collective-permute-start(bf16[2,2,512,512]{3,2,1,0:T(8,128)(2,1)} %collective-permute-done.2), channel_id=1, source_target_pairs={{2,0},{4,2},{6,4},{8,6},{10,8},{12,10},{14,12},{16,14},{18,16},{20... | collective-permute-start | bytes 6291464 | tf_op jit(solution)/shard_map/ppermute | solution.py:10
  161.7 4.2 %copy-start.7 = (f32[512,512]{0,1:T(8,128)}, f32[512,512]{0,1:T(8,128)S(1)}, u32[]{:S(2)}) copy-start(f32[512,512]{0,1:T(8,128)S(1)} %get-tuple-element.48) | copy-start | bytes 3145732
  174.8 6.0 %copy-start.12 = (f32[512,512]{1,0:T(8,128)S(1)}, f32[512,512]{1,0:T(8,128)}, u32[]{:S(2)}) copy-start(f32[512,512]{1,0:T(8,128)} %copy.138) | copy-start | bytes 3145732
  210.8 2.7 %copy-start.6 = (f32[512,512]{0,1:T(8,128)S(1)}, f32[512,512]{0,1:T(8,128)}, u32[]{:S(2)}) copy-start(f32[512,512]{0,1:T(8,128)} %get-tuple-element.55) | copy-start | bytes 3145732
  210.8 2.7 %copy-start.13 = (f32[512,512]{1,0:T(8,128)S(1)}, f32[512,512]{1,0:T(8,128)}, u32[]{:S(2)}) copy-start(f32[512,512]{1,0:T(8,128)} %copy.148) | copy-start | bytes 3145732
  210.8 5.0 %copy-start.8 = (f32[512,512]{0,1:T(8,128)S(1)}, f32[512,512]{0,1:T(8,128)}, u32[]{:S(2)}) copy-start(f32[512,512]{0,1:T(8,128)} %get-tuple-element.56) | copy-start | bytes 3145732
  210.8 5.0 %copy-start.9 = (f32[512,512]{0,1:T(8,128)S(1)}, f32[512,512]{0,1:T(8,128)}, u32[]{:S(2)}) copy-start(f32[512,512]{0,1:T(8,128)} %get-tuple-element.57) | copy-start | bytes 3145732
  210.8 5.0 %copy-start.14 = (f32[512,512]{1,0:T(8,128)S(1)}, f32[512,512]{1,0:T(8,128)}, u32[]{:S(2)}) copy-start(f32[512,512]{1,0:T(8,128)} %copy.150) | copy-start | bytes 3145732
  210.9 5.0 %copy-start.15 = (f32[512,512]{1,0:T(8,128)S(1)}, f32[512,512]{1,0:T(8,128)}, u32[]{:S(2)}) copy-start(f32[512,512]{1,0:T(8,128)} %copy.151) | copy-start | bytes 3145732
Sparse Core Ops, SparseCore 0:
  9.5 59.4 all-gather.2
where the time goes:
time: 263 us; the launch traced here: 262 us
  other arithmetic  55.3 us (21%)
  local copies, waits for them, and re-layouts  49.5 us (19%)
  between operations  41 us (16%)
  waiting for transfers between devices  37.2 us (14%)
  matrix products  33 us (13%)
  blocking collectives  30.3 us (12%)
  starting transfers between devices  15.3 us (6%)
    dot_general x12, matrix products, products(): jnp.einsum('xij,yjk->xyik', source, target, preferred_element_type=jnp.fl...  33 us
    reduce_sum x12, other arithmetic, products(): direct = jnp.trace(real_part)  31.1 us
    psum x1, blocking collectives, record(): totals.append(lax.psum(result, 'tm'))  30.3 us
    sub x12, local copies, waits for them, and re-layouts, products(): real_part = product_full[0, 0] - product_full[1, 1]  25.2 us
    ppermute x4, waiting for transfers between devices, from_behind(): return lax.ppermute(block, axis, route)  23.9 us
    add x12, local copies, waits for them, and re-layouts, products(): imag_part = product_full[0, 1] + product_full[1, 0]  20.9 us
    ppermute x4, starting transfers between devices, from_behind(): return lax.ppermute(block, axis, route)  15.2 us
    add x12, other arithmetic, products(): imag_part = product_full[0, 1] + product_full[1, 0]  14.5 us
  transfers between devices with their start and end apart: 5, of which 2 were waited for; matrix products, arithmetic and copies ran while one was open for 33% of the time, Pallas kernels for 0%

commit v1 on v0

v1 whole, which is shorter than its diff:
```python
import functools

import jax
import jax.numpy as jnp
from jax import lax
from jax.experimental import pallas as pl
from jax.experimental.pallas import tpu as pltpu
from jax.sharding import PartitionSpec as P

MESH = pl.DeviceIdType.MESH
BLK = 128


def kernel(n_tm, n_mom, pair_ref, field_ref, local_ref, sum_ref, *scratch):
    per_group, _, nev, _ = field_ref.shape[1:]
    stages = nev // BLK
    slots = 4
    subs = per_group * 2
    pairs = pair_ref.shape[0]
    a_bufs = scratch[:stages]
    b_flat = scratch[stages : stages + stages * slots]
    b_bufs = [b_flat[n * slots : (n + 1) * slots] for n in range(stages)]
    acc_d, acc_b, gathered = scratch[stages + stages * slots : stages + stages * slots + 3]
    own_sem, y_send, y_recv, b_send, b_recv, r_send, r_recv = scratch[-7:]

    me = lax.axis_index("tm")
    group = lax.axis_index("mom")

    def at(step):
        return {"tm": lax.rem(me + step + n_tm, n_tm), "mom": group}

    upper_core = lax.rem(me, 2) == 1
    odd_chip = lax.rem(me // 2, 2) == 1

    own_copies = []
    for n in range(stages):
        copy = pltpu.make_async_copy(
            field_ref.at[0, :, :, pl.ds(n * BLK, BLK), :],
            a_bufs[n].at[pl.ds(group * per_group, per_group)],
            own_sem.at[n],
        )
        copy.start()
        own_copies.append(copy)

    barrier = pltpu.get_barrier_semaphore()

    def greet(i, carry):
        pl.semaphore_signal(barrier, inc=1, device_id=at(i), device_id_type=MESH)
        return carry

    lax.fori_loop(1, n_tm, greet, 0)
    for j in range(1, n_mom):
        pl.semaphore_signal(
            barrier, inc=1, device_id={"tm": me, "mom": lax.rem(group + j, n_mom)}, device_id_type=MESH
        )
    pl.semaphore_wait(barrier, n_tm - 1 + n_mom - 1)

    def own_part(n, sub):
        return field_ref.at[0, sub // 2, sub % 2, :, pl.ds(n * BLK, BLK)]

    def part(n, slot, sub):
        return b_bufs[n][slot - 1].at[sub // 2, sub % 2]

    def hop(src, n, slot, sub, step):
        return pltpu.make_async_remote_copy(
            src_ref=src,
            dst_ref=part(n, slot, sub),
            send_sem=b_send.at[slot - 1, n, sub],
            recv_sem=b_recv.at[slot - 1, n, sub],
            device_id=at(step),
            device_id_type=MESH,
        )

    def across(n, j):
        return pltpu.make_async_remote_copy(
            src_ref=field_ref.at[0, :, :, pl.ds(n * BLK, BLK), :],
            dst_ref=a_bufs[n].at[pl.ds(group * per_group, per_group)],
            send_sem=y_send.at[n, j],
            recv_sem=y_recv.at[n, j],
            device_id={"tm": me, "mom": lax.rem(group + j, n_mom)},
            device_id_type=MESH,
        )

    for n in range(stages):
        for j in range(1, n_mom):
            across(n, j).start()
        for sub in range(subs):
            hop(own_part(n, sub), n, 4, sub, -4).start()

        @pl.when(odd_chip)
        def _():
            for sub in range(subs):
                hop(own_part(n, sub), n, 2, sub, -2).start()

        @pl.when(upper_core)
        def _():
            for sub in range(subs):
                hop(own_part(n, sub), n, 1, sub, -1).start()

    def relay(n, sub):
        hop(part(n, 4, sub), n, 4, sub, -4).wait_recv()

        @pl.when(jnp.logical_not(odd_chip))
        def _():
            hop(part(n, 4, sub), n, 2, sub, 2).start()

        @pl.when(jnp.logical_not(upper_core))
        def _():
            hop(part(n, 4, sub), n, 3, sub, 1).start()

        hop(part(n, 2, sub), n, 2, sub, -2).wait_recv()

        @pl.when(upper_core)
        def _():
            hop(part(n, 2, sub), n, 3, sub, -1).start()

        @pl.when(jnp.logical_not(upper_core))
        def _():
            hop(part(n, 2, sub), n, 1, sub, 1).start()

    acc_d[...] = jnp.zeros_like(acc_d)
    acc_b[...] = jnp.zeros_like(acc_b)
    eye = (
        lax.broadcasted_iota(jnp.int32, (BLK, BLK), 0) == lax.broadcasted_iota(jnp.int32, (BLK, BLK), 1)
    ).astype(jnp.float32)

    def fold(x):
        return jnp.sum(x.reshape(BLK // 8, 8, BLK), axis=0)

    def compute(n, slot):
        def body(k, carry):
            a = pair_ref[k, 0]
            b = lax.rem(pair_ref[k, 1], per_group)

            def left(i):
                return jnp.concatenate([a_bufs[i][a, 0], a_bufs[i][a, 1]], axis=1)

            def right(i):
                buf = b_bufs[i][slot - 1]
                re, im = buf[b, 0], buf[b, 1]
                return jnp.concatenate(
                    [jnp.concatenate([re, im], axis=1), jnp.concatenate([-im, re], axis=1)], axis=0
                )

            lhs = left(n)
            column = jnp.dot(
                jnp.concatenate([left(i) for i in range(n)] + [lhs], axis=0),
                right(n),
                preferred_element_type=jnp.float32,
            )
            box = jnp.zeros((BLK, BLK), jnp.float32)
            for j in range(n):
                row = jnp.dot(lhs, right(j), preferred_element_type=jnp.float32)
                upper = column[j * BLK : (j + 1) * BLK]
                box += upper[:, :BLK] * row[:, :BLK].T - upper[:, BLK:] * row[:, BLK:].T
            corner = column[n * BLK :]
            re, im = corner[:, :BLK], corner[:, BLK:]
            box = box + box + re * re.T - im * im.T
            index = (slot - 1) * pairs + k
            acc_b[index] += fold(box)
            acc_d[index] += fold(re * eye)
            return carry

        lax.fori_loop(0, pairs, body, 0)

    for sub in range(subs):
        relay(0, sub)
    for n in range(stages):
        own_copies[n].wait()
        for j in range(1, n_mom):
            across(n, j).wait_recv()
        for place, slot in enumerate((4, 2, 1, 3)):
            if slot % 2 == 1:
                for sub in range(subs):
                    hop(part(n, slot, sub), n, slot, sub, -1).wait_recv()
            compute(n, slot)
            if n + 1 < stages:
                for sub in range(place * subs // slots, (place + 1) * subs // slots):
                    relay(n + 1, sub)

    def lanes(acc):
        count = acc.shape[0]
        each = jnp.sum(jnp.sum(acc[...], axis=1), axis=1, keepdims=True)
        row = lax.broadcasted_iota(jnp.int32, (count, BLK), 0)
        lane = lax.broadcasted_iota(jnp.int32, (count, BLK), 1)
        return jnp.sum(jnp.where(row == lane, jnp.broadcast_to(each, (count, BLK)), 0.0), axis=0, keepdims=True)

    which = lax.broadcasted_iota(jnp.int32, (8, BLK), 0)
    stat = jnp.where(which == 0, lanes(acc_d), jnp.where(which == 1, lanes(acc_b), 0.0))
    gathered[me] = stat
    local_ref[...] = stat

    def give(i):
        return pltpu.make_async_remote_copy(
            src_ref=gathered.at[me],
            dst_ref=gathered.at[me],
            send_sem=r_send.at[i],
            recv_sem=r_recv.at[i],
            device_id=at(i),
            device_id_type=MESH,
        )

    def start_give(i, carry):
        give(i).start()
        return carry

    lax.fori_loop(1, n_tm, start_give, 0)
    for n in range(stages):
        for j in range(1, n_mom):
            across(n, j).wait_send()
        for sub in range(subs):
            for slot in range(1, slots + 1):
                hop(part(n, slot, sub), n, slot, sub, -1).wait_send()

    def end_give(i, carry):
        give(i).wait()
        return carry

    lax.fori_loop(1, n_tm, end_give, 0)
    sum_ref[...] = jnp.sum(gathered[...], axis=0)


def reorder(stacked, deltas):
    picker = (deltas[:, None] == jnp.arange(deltas.shape[0], dtype=jnp.int32)[None, :]).astype(
        jnp.float32
    )
    return jnp.sum(picker[:, :, None] * stacked[..., None, :, :], axis=-2)


def per_device(n_tm, n_mom, fields, mom_pairs, deltas):
    _, per_group, _, nev, _ = fields.shape
    pairs = mom_pairs.shape[0]
    seps = deltas.shape[0]
    stages = nev // BLK
    subs = per_group * 2
    slots = 4
    rows = -(-seps * pairs // 8) * 8
    scratch = (
        [pltpu.VMEM((n_mom * per_group, 2, BLK, nev), fields.dtype)] * stages
        + [pltpu.VMEM((per_group, 2, nev, BLK), fields.dtype)] * (stages * slots)
        + [pltpu.VMEM((rows, 8, BLK), jnp.float32)] * 2
        + [pltpu.VMEM((n_tm, 8, BLK), jnp.float32)]
        + [
            pltpu.SemaphoreType.DMA((stages,)),
            pltpu.SemaphoreType.DMA((stages, n_mom)),
            pltpu.SemaphoreType.DMA((stages, n_mom)),
            pltpu.SemaphoreType.DMA((slots, stages, subs)),
            pltpu.SemaphoreType.DMA((slots, stages, subs)),
            pltpu.SemaphoreType.DMA((n_tm,)),
            pltpu.SemaphoreType.DMA((n_tm,)),
        ]
    )
    tile = jax.ShapeDtypeStruct((8, BLK), jnp.float32)
    local, total = pl.pallas_call(
        functools.partial(kernel, n_tm, n_mom),
        out_shape=(tile, tile),
        in_specs=[pl.BlockSpec(memory_space=pltpu.SMEM), pl.BlockSpec(memory_space=pl.ANY)],
        out_specs=(pl.BlockSpec(memory_space=pltpu.VMEM), pl.BlockSpec(memory_space=pltpu.VMEM)),
        scratch_shapes=scratch,
        compiler_params=pltpu.CompilerParams(
            collective_id=0, has_side_effects=True, vmem_limit_bytes=48 * 1024 * 1024
        ),
    )(mom_pairs, fields)

    def unpack(x):
        return reorder(x[:2, : seps * pairs].reshape(2, seps, pairs), deltas)

    return (unpack(local)[None], unpack(total))


def solution(mesh):
    return jax.shard_map(
        functools.partial(per_device, mesh.shape["tm"], mesh.shape["mom"]),
        mesh=mesh,
        in_specs=(P("tm", "mom", None, None, None), P("mom", None), P()),
        out_specs=(P("tm", None, None, "mom"), P(None, None, "mom")),
        check_vma=False,
    )
```

time: 263 us -> 79.5 us (0.30)
  Pallas kernels: 0 us -> 74 us
  other arithmetic: 55.3 us -> 0.82 us
  local copies, waits for them, and re-layouts: 49.5 us -> 3.89 us
  between operations: 41 us -> 0.66 us
  waiting for transfers between devices: 37.2 us -> 0 us
  matrix products: 33 us -> 0 us
  blocking collectives: 30.3 us -> 0 us
  starting transfers between devices: 15.3 us -> 0 us
    pallas_call x0 -> x1, Pallas kernels: none -> 74 us  [per_device(): pl.pallas_call(functools.partial(kernel, n_tm, n_mom), out_shape=(tile, t...]
    dot_general x12 -> x0, matrix products: 33 us -> none  [products(): jnp.einsum('xij,yjk->xyik', source, target, preferred_element_type=jnp.fl...]
    reduce_sum x12 -> x0, other arithmetic: 31.1 us -> none  [products(): direct = jnp.trace(real_part)]
    psum x1 -> x0, blocking collectives: 30.3 us -> none  [record(): totals.append(lax.psum(result, 'tm'))]
    sub x12 -> x0, local copies, waits for them, and re-layouts: 25.2 us -> none  [products(): real_part = product_full[0, 0] - product_full[1, 1]]
    ppermute x4 -> x0, waiting for transfers between devices: 23.9 us -> none  [from_behind(): return lax.ppermute(block, axis, route)]
    add x12 -> x0, local copies, waits for them, and re-layouts: 20.9 us -> none  [products(): imag_part = product_full[0, 1] + product_full[1, 0]]
    ppermute x4 -> x0, starting transfers between devices: 15.2 us -> none  [from_behind(): return lax.ppermute(block, axis, route)]
  transfers between devices with their start and end apart: 5 -> 0, of which waited for: 2 -> 0; matrix products, arithmetic and copies ran while one was open for 33% -> 0% of each run, Pallas kernels for 0% -> 0%
where the time goes in v1:
time: 79.5 us; the launch traced here: 79.3 us
  Pallas kernels  74 us (93%)
  local copies, waits for them, and re-layouts  3.89 us (5%)
  other arithmetic  0.82 us (1%)
    pallas_call x1, Pallas kernels, per_device(): pl.pallas_call(functools.partial(kernel, n_tm, n_mom), out_shape=(tile, t...  74 us
    unnamed x4, local copies, waits for them, and re-layouts  2.94 us

profile of v1, /device:TPU:0, one launch (start us, length us, event | category | flops | bytes accessed | tf_op | source)
XLA Modules:
  0.0 79.3 jit_solution(7249385541468330763)
XLA Ops:
  0.6 0.8 copy.7.pair_ref
  1.4 0.7 fusion
  2.1 0.0 copy-start
  2.1 1.6 %copy-done = bf16[1,2,2,512,512]{4,3,2,1,0:T(8,128)(2,1)S(1)} copy-done((bf16[1,2,2,512,512]{4,3,2,1,0:T(8,128)(2,1)S(1)}, bf16[1,2,2,512,512]{4,3,2,1,0:T(8,128)(2,1)}, u32[]{:S(2)}) %copy-start) | copy-done | bytes 2097176
  3.7 74.0 %shard_map.50 = (f32[8,128]{1,0:T(8,128)S(1)}, f32[8,128]{1,0:T(8,128)S(1)}) custom-call(s32[3,2]{1,0:T(4,128)S(1)} %copy.7.pair_ref, bf16[1,2,2,512,512]{4,3,2,1,0:T(8,128)(2,1)S(1)} %copy-done), custom_call_target="tpu_custom_call" | custom-call | tf_op jit(solution)/shard_map/pallas_call | solution.py:254
  77.7 0.1 mul.32
  77.8 0.1 copy.10
  77.9 0.1 mul.29
  78.0 0.1 copy.8
  78.1 0.1 multiply_reduce_fusion
  78.2 0.6 copy.11
  78.8 0.6 copy.13
  (2 shorter events, 0.0 us)
Async XLA Ops:
  2.1 1.6 %copy-start = (bf16[1,2,2,512,512]{4,3,2,1,0:T(8,128)(2,1)S(1)}, bf16[1,2,2,512,512]{4,3,2,1,0:T(8,128)(2,1)}, u32[]{:S(2)}) copy-start(bf16[1,2,2,512,512]{4,3,2,1,0:T(8,128)(2,1)} %field_ref.1) | copy-start | bytes 6291460

commit v2 on v1

--- a/solution.py
+++ b/solution.py
@@ -11,16 +11,17 @@
 BLK = 128
 
 
-def kernel(n_tm, n_mom, pair_ref, field_ref, local_ref, sum_ref, *scratch):
+def kernel(n_tm, n_mom, pair_ref, delta_ref, field_ref, local_ref, sum_ref, *scratch):
     per_group, _, nev, _ = field_ref.shape[1:]
     stages = nev // BLK
     slots = 4
     subs = per_group * 2
-    pairs = pair_ref.shape[0]
+    pairs = pair_ref.shape[1]
+    seps = delta_ref.shape[0]
     a_bufs = scratch[:stages]
     b_flat = scratch[stages : stages + stages * slots]
     b_bufs = [b_flat[n * slots : (n + 1) * slots] for n in range(stages)]
-    acc_d, acc_b, gathered = scratch[stages + stages * slots : stages + stages * slots + 3]
+    acc_d, acc_b, held, gathered = scratch[stages + stages * slots : stages + stages * slots + 4]
     own_sem, y_send, y_recv, b_send, b_recv, r_send, r_recv = scratch[-7:]
 
     me = lax.axis_index("tm")
@@ -97,7 +98,7 @@
             for sub in range(subs):
                 hop(own_part(n, sub), n, 1, sub, -1).start()
 
-    def relay(n, sub):
+    def relay_four(n, sub):
         hop(part(n, 4, sub), n, 4, sub, -4).wait_recv()
 
         @pl.when(jnp.logical_not(odd_chip))
@@ -108,6 +109,7 @@
         def _():
             hop(part(n, 4, sub), n, 3, sub, 1).start()
 
+    def relay_two(n, sub):
         hop(part(n, 2, sub), n, 2, sub, -2).wait_recv()
 
         @pl.when(upper_core)
@@ -127,68 +129,93 @@
     def fold(x):
         return jnp.sum(x.reshape(BLK // 8, 8, BLK), axis=0)
 
-    def compute(n, slot):
-        def body(k, carry):
-            a = pair_ref[k, 0]
-            b = lax.rem(pair_ref[k, 1], per_group)
-
-            def left(i):
-                return jnp.concatenate([a_bufs[i][a, 0], a_bufs[i][a, 1]], axis=1)
-
-            def right(i):
-                buf = b_bufs[i][slot - 1]
-                re, im = buf[b, 0], buf[b, 1]
-                return jnp.concatenate(
-                    [jnp.concatenate([re, im], axis=1), jnp.concatenate([-im, re], axis=1)], axis=0
-                )
-
-            lhs = left(n)
+    def left(i, k):
+        a = pair_ref[0, k]
+        return jnp.concatenate([a_bufs[i][a, 0], a_bufs[i][a, 1]], axis=1)
+
+    def right(i, slot, k):
+        b = lax.rem(pair_ref[1, k], per_group)
+        buf = b_bufs[i][slot - 1]
+        re, im = buf[b, 0], buf[b, 1]
+        return jnp.concatenate(
+            [jnp.concatenate([re, im], axis=1), jnp.concatenate([-im, re], axis=1)], axis=0
+        )
+
+    def rows_of(n, slot):
+        for k in range(pairs):
+            lhs = left(n, k)
+            for j in range(n):
+                row = jnp.dot(lhs, right(j, slot, k), preferred_element_type=jnp.float32)
+                index = (slot - 1) * pairs + k
+                held[index, j, 0] = row[:, :BLK].T
+                held[index, j, 1] = row[:, BLK:].T
+
+    def columns_of(n, slot):
+        for k in range(pairs):
+            index = (slot - 1) * pairs + k
             column = jnp.dot(
-                jnp.concatenate([left(i) for i in range(n)] + [lhs], axis=0),
-                right(n),
+                jnp.concatenate([left(i, k) for i in range(n + 1)], axis=0),
+                right(n, slot, k),
                 preferred_element_type=jnp.float32,
             )
             box = jnp.zeros((BLK, BLK), jnp.float32)
             for j in range(n):
-                row = jnp.dot(lhs, right(j), preferred_element_type=jnp.float32)
                 upper = column[j * BLK : (j + 1) * BLK]
-                box += upper[:, :BLK] * row[:, :BLK].T - upper[:, BLK:] * row[:, BLK:].T
+                box += upper[:, :BLK] * held[index, j, 0] - upper[:, BLK:] * held[index, j, 1]
             corner = column[n * BLK :]
             re, im = corner[:, :BLK], corner[:, BLK:]
             box = box + box + re * re.T - im * im.T
-            index = (slot - 1) * pairs + k
             acc_b[index] += fold(box)
             acc_d[index] += fold(re * eye)
-            return carry
-
-        lax.fori_loop(0, pairs, body, 0)
-
+
+    order = (4, 2, 1, 3)
+    share = [range(p * subs // slots, (p + 1) * subs // slots) for p in range(slots)]
+    late = share[-1]
     for sub in range(subs):
-        relay(0, sub)
+        relay_four(0, sub)
+        relay_two(0, sub)
     for n in range(stages):
         own_copies[n].wait()
         for j in range(1, n_mom):
             across(n, j).wait_recv()
-        for place, slot in enumerate((4, 2, 1, 3)):
+        if n:
+            for slot in order[: slots // 2]:
+                rows_of(n, slot)
+            for sub in late:
+                relay_two(n, sub)
+            for slot in order[slots // 2 :]:
+                rows_of(n, slot)
+        for place, slot in enumerate(order):
             if slot % 2 == 1:
                 for sub in range(subs):
                     hop(part(n, slot, sub), n, slot, sub, -1).wait_recv()
-            compute(n, slot)
+            columns_of(n, slot)
             if n + 1 < stages:
-                for sub in range(place * subs // slots, (place + 1) * subs // slots):
-                    relay(n + 1, sub)
-
-    def lanes(acc):
-        count = acc.shape[0]
+                for sub in share[place]:
+                    relay_four(n + 1, sub)
+                    if place < slots - 1:
+                        relay_two(n + 1, sub)
+
+    count = acc_d.shape[0]
+    height = gathered.shape[1]
+    lane = lax.broadcasted_iota(jnp.int32, (1, BLK), 1)
+    wanted = jnp.zeros((1, BLK), jnp.int32)
+    for r in range(seps):
+        wanted = jnp.where(lane == r, delta_ref[r], wanted)
+    index = lax.broadcasted_iota(jnp.int32, (count, BLK), 0)
+    which = lax.broadcasted_iota(jnp.int32, (height, BLK), 0)
+    stat = jnp.zeros((height, BLK), jnp.float32)
+    for p, acc in enumerate((acc_d, acc_b)):
         each = jnp.sum(jnp.sum(acc[...], axis=1), axis=1, keepdims=True)
-        row = lax.broadcasted_iota(jnp.int32, (count, BLK), 0)
-        lane = lax.broadcasted_iota(jnp.int32, (count, BLK), 1)
-        return jnp.sum(jnp.where(row == lane, jnp.broadcast_to(each, (count, BLK)), 0.0), axis=0, keepdims=True)
-
-    which = lax.broadcasted_iota(jnp.int32, (8, BLK), 0)
-    stat = jnp.where(which == 0, lanes(acc_d), jnp.where(which == 1, lanes(acc_b), 0.0))
+        each = jnp.broadcast_to(each, (count, BLK))
+        for k in range(pairs):
+            line = jnp.sum(jnp.where(index == wanted * pairs + k, each, 0.0), axis=0, keepdims=True)
+            stat = jnp.where(which == 2 * k + p, jnp.broadcast_to(line, (height, BLK)), stat)
     gathered[me] = stat
-    local_ref[...] = stat
+
+    def write(ref, value):
+        for k in range(pairs):
+            ref[k] = value[2 * k : 2 * k + 2, :seps]
 
     def give(i):
         return pltpu.make_async_remote_copy(
@@ -200,11 +227,10 @@
             device_id_type=MESH,
         )
 
-    def start_give(i, carry):
+    far = sorted(range(1, n_tm), key=lambda i: -min(i, n_tm - i))
+    for i in far:
         give(i).start()
-        return carry
-
-    lax.fori_loop(1, n_tm, start_give, 0)
+    write(local_ref, stat)
     for n in range(stages):
         for j in range(1, n_mom):
             across(n, j).wait_send()
@@ -212,19 +238,9 @@
             for slot in range(1, slots + 1):
                 hop(part(n, slot, sub), n, slot, sub, -1).wait_send()
 
-    def end_give(i, carry):
+    for i in reversed(far):
         give(i).wait()
-        return carry
-
-    lax.fori_loop(1, n_tm, end_give, 0)
-    sum_ref[...] = jnp.sum(gathered[...], axis=0)
-
-
-def reorder(stacked, deltas):
-    picker = (deltas[:, None] == jnp.arange(deltas.shape[0], dtype=jnp.int32)[None, :]).astype(
-        jnp.float32
-    )
-    return jnp.sum(picker[:, :, None] * stacked[..., None, :, :], axis=-2)
+    write(sum_ref, jnp.sum(gathered[...], axis=0))
 
 
 def per_device(n_tm, n_mom, fields, mom_pairs, deltas):
@@ -235,11 +251,13 @@
     subs = per_group * 2
     slots = 4
     rows = -(-seps * pairs // 8) * 8
+    height = -(-2 * pairs // 8) * 8
     scratch = (
         [pltpu.VMEM((n_mom * per_group, 2, BLK, nev), fields.dtype)] * stages
         + [pltpu.VMEM((per_group, 2, nev, BLK), fields.dtype)] * (stages * slots)
         + [pltpu.VMEM((rows, 8, BLK), jnp.float32)] * 2
-        + [pltpu.VMEM((n_tm, 8, BLK), jnp.float32)]
+        + [pltpu.VMEM((rows, stages - 1, 2, BLK, BLK), jnp.float32)]
+        + [pltpu.VMEM((n_tm, height, BLK), jnp.float32)]
         + [
             pltpu.SemaphoreType.DMA((stages,)),
             pltpu.SemaphoreType.DMA((stages, n_mom)),
@@ -250,22 +268,23 @@
             pltpu.SemaphoreType.DMA((n_tm,)),
         ]
     )
-    tile = jax.ShapeDtypeStruct((8, BLK), jnp.float32)
+    tile = jax.ShapeDtypeStruct((pairs, 2, seps), jnp.float32)
     local, total = pl.pallas_call(
         functools.partial(kernel, n_tm, n_mom),
         out_shape=(tile, tile),
-        in_specs=[pl.BlockSpec(memory_space=pltpu.SMEM), pl.BlockSpec(memory_space=pl.ANY)],
+        in_specs=[
+            pl.BlockSpec(memory_space=pltpu.SMEM),
+            pl.BlockSpec(memory_space=pltpu.SMEM),
+            pl.BlockSpec(memory_space=pltpu.HBM),
+        ],
         out_specs=(pl.BlockSpec(memory_space=pltpu.VMEM), pl.BlockSpec(memory_space=pltpu.VMEM)),
         scratch_shapes=scratch,
         compiler_params=pltpu.CompilerParams(
-            collective_id=0, has_side_effects=True, vmem_limit_bytes=48 * 1024 * 1024
+            collective_id=0, has_side_effects=True, vmem_limit_bytes=67_043_328
         ),
-    )(mom_pairs, fields)
-
-    def unpack(x):
-        return reorder(x[:2, : seps * pairs].reshape(2, seps, pairs), deltas)
-
-    return (unpack(local)[None], unpack(total))
+    )(mom_pairs.T, deltas, fields)
+
+    return (local.transpose(1, 2, 0)[None], total.transpose(1, 2, 0))
 
 
 def solution(mesh):

time: 79.5 us -> 75.9 us (0.955)
  Pallas kernels: 74 us -> 72.6 us
  local copies, waits for them, and re-layouts: 3.89 us -> 2.49 us
  other arithmetic: 0.82 us -> 0 us
    pallas_call x1, Pallas kernels: 74 us -> 72.6 us  [per_device(): pl.pallas_call(functools.partial(kernel, n_tm, n_mom), out_shape=(tile, t...]
    unnamed x4 -> x2, local copies, waits for them, and re-layouts: 2.94 us -> 2.49 us
where the time goes in v2:
time: 75.9 us; the launch traced here: 75.7 us
  Pallas kernels  72.6 us (96%)
  local copies, waits for them, and re-layouts  2.49 us (3%)
    pallas_call x1, Pallas kernels, per_device(): pl.pallas_call(functools.partial(kernel, n_tm, n_mom), out_shape=(tile, t...  72.6 us
    unnamed x2, local copies, waits for them, and re-layouts  2.49 us

profile of v2, /device:TPU:0, one launch (start us, length us, event | category | flops | bytes accessed | tf_op | source)
XLA Modules:
  0.0 75.7 jit_solution(915643534377868664)
XLA Ops:
  0.6 72.6 %shard_map.50 = (f32[3,2,4]{2,1,0:T(2,128)}, f32[3,2,4]{2,1,0:T(2,128)}) custom-call(s32[2,3]{1,0:T(2,128)} %bitcast.7, s32[4]{0:T(128)} %delta_ref.1, bf16[1,2,2,512,512]{4,3,2,1,0:T(8,128)(2,1)} %field_ref.1), custom_call_target="tpu_custom_call" | custom-call | tf_op jit(solution)/shard_map/pallas_call | solution.py:272
  73.2 1.3 %copy.7 = f32[1,2,4,3]{2,1,3,0:T(2,128)} copy(f32[1,2,4,3]{2,1,3,0:T(2,128)} %bitcast.6) | data formatting | bytes 192
  74.4 1.2 %copy.8 = f32[2,4,3]{1,0,2:T(2,128)} copy(f32[2,4,3]{1,0,2:T(2,128)} %bitcast.5) | data formatting | bytes 192
